TPU v7x, 8 devices: a whole 2x2x1 slice. The times are simulated.
8 devices in a mesh: batch: 1 (over z), gz: 2 (over y), gy: 2 (over x), gx: 2 (over core).
Axes of the slice: x: 2, y: 2, z: 1, core: 2. Of those that a mesh axis runs over, the one named last changes fastest.
Arguments:
- rhs_grid: float32 [256, 256, 256], P(('batch', 'gz'), 'gy', 'gx')
- init_grid: float32 [256, 256, 256], P(('batch', 'gz'), 'gy', 'gx')
- coarse_inv: float32 [64, 64], replicated
Outputs:
- output: float32 [256, 256, 256], P(('batch', 'gz'), 'gy', 'gx')
All inputs are finite; a program needn't handle non-finite values.
Results may differ from a plain program's by a relative error of at most 0.001.
Values sent between devices are 32-bit elements.
A program may use at most 1 GiB of HBM per device.

v0:
```python
import jax
import jax.numpy as jnp
from jax import lax
from jax.sharding import PartitionSpec as P

OMEGA = 2.0 / 3.0
CYCLES = 2
SWEEPS = 2
GRID_AXES = ('gz', 'gy', 'gx')


def solution(mesh):
    axis_lens = tuple(mesh.shape[axis_name] for axis_name in GRID_AXES)
    grid_spec = P(('batch', 'gz'), 'gy', 'gx')

    def with_ghosts(iterate, axis_id):
        extent = iterate.shape[axis_id]
        first_face = lax.slice_in_dim(iterate, 0, 1, axis=axis_id)
        last_face = lax.slice_in_dim(iterate, extent - 1, extent, axis=axis_id)
        axis_name = GRID_AXES[axis_id]
        axis_len = axis_lens[axis_id]
        if axis_len == 1:
            low_ghost = -first_face
            high_ghost = -last_face
        else:
            from_below = lax.ppermute(last_face, axis_name, [(src_id, src_id + 1) for src_id in range(axis_len - 1)])
            from_above = lax.ppermute(first_face, axis_name, [(src_id + 1, src_id) for src_id in range(axis_len - 1)])
            position = lax.axis_index(axis_name)
            low_ghost = jnp.where(position == 0, -first_face, from_below)
            high_ghost = jnp.where(position == axis_len - 1, -last_face, from_above)
        return jnp.concatenate([low_ghost, iterate, high_ghost], axis=axis_id)

    def neighbour_sum(iterate):
        nbr_total = jnp.zeros_like(iterate)
        for axis_id in range(3):
            extent = iterate.shape[axis_id]
            padded = with_ghosts(iterate, axis_id)
            nbr_total = nbr_total + lax.slice_in_dim(padded, 0, extent, axis=axis_id) + lax.slice_in_dim(padded, 2, extent + 2, axis=axis_id)
        return nbr_total

    def jacobi(iterate, source, edge_cells):
        return (1.0 - OMEGA) * iterate + (OMEGA / 6.0) * (source * (1.0 / (edge_cells * edge_cells)) + neighbour_sum(iterate))

    def residual(iterate, source, edge_cells):
        return source - (6.0 * iterate - neighbour_sum(iterate)) * float(edge_cells * edge_cells)

    def restrict(fine_grid):
        dim_z, dim_y, dim_x = fine_grid.shape
        return fine_grid.reshape(dim_z // 2, 2, dim_y // 2, 2, dim_x // 2, 2).mean(axis=(1, 3, 5))

    def prolong(coarse):
        for axis_id in range(3):
            extent = coarse.shape[axis_id]
            padded = with_ghosts(coarse, axis_id)
            low_child = 0.75 * coarse + 0.25 * lax.slice_in_dim(padded, 0, extent, axis=axis_id)
            high_child = 0.75 * coarse + 0.25 * lax.slice_in_dim(padded, 2, extent + 2, axis=axis_id)
            new_shape = list(coarse.shape)
            new_shape[axis_id] = 2 * extent
            coarse = jnp.stack([low_child, high_child], axis=axis_id + 1).reshape(new_shape)
        return coarse

    def coarse_solve(source, coarse_inv):
        gathered = lax.all_gather(source, 'gx', axis=2, tiled=True)
        gathered = lax.all_gather(gathered, 'gy', axis=1, tiled=True)
        gathered = lax.all_gather(gathered, 'gz', axis=0, tiled=True)
        solved = jnp.dot(coarse_inv, gathered.reshape(-1), precision=lax.Precision.HIGHEST).reshape(gathered.shape)
        starts = tuple(lax.axis_index(GRID_AXES[axis_id]) * source.shape[axis_id] for axis_id in range(3))
        return lax.dynamic_slice(solved, starts, source.shape)

    def vcycle(iterate, source, coarse_inv, coarse_edge):
        edge_cells = iterate.shape[0] * axis_lens[0]
        if edge_cells == coarse_edge:
            return coarse_solve(source, coarse_inv)
        for sweep_id in range(SWEEPS):
            iterate = jacobi(iterate, source, edge_cells)
        coarse_rhs = restrict(residual(iterate, source, edge_cells))
        correction = vcycle(jnp.zeros_like(coarse_rhs), coarse_rhs, coarse_inv, coarse_edge)
        iterate = iterate + prolong(correction)
        for sweep_id in range(SWEEPS):
            iterate = jacobi(iterate, source, edge_cells)
        return iterate

    def local_cycles(rhs_grid, init_grid, coarse_inv):
        coarse_edge = int(round(coarse_inv.shape[0] ** (1.0 / 3.0)))
        iterate = init_grid
        for cycle_id in range(CYCLES):
            iterate = vcycle(iterate, rhs_grid, coarse_inv, coarse_edge)
        return iterate

    return jax.shard_map(local_cycles, mesh=mesh, in_specs=(grid_spec, grid_spec, P()), out_specs=grid_spec, check_vma=False)
```

profile of v0, /device:TPU:0, one launch (start us, length us, event | category | flops | bytes accessed | tf_op | source)
XLA Modules:
  0.0 4130.4 jit_solution(8859124337436335316)
XLA Ops:
  12.3 9.3 copy.673
  21.6 13.2 fusion.679
  47.5 9.4 copy.674
  184.6 16.0 negate_select_fusion.19
  202.9 32.4 fusion.75
  235.3 8.1 fusion.676
  280.5 16.0 negate_select_fusion.17
  298.8 32.4 fusion.67
  376.1 16.0 negate_select_fusion.15
  394.4 32.4 fusion.59
  426.8 9.3 copy.700
  436.1 538.7 %reshape.154 = f32[64,2,64,2,64,2]{5,4,3,2,1,0:T(8,128)} reshape(f32[128,128,128]{2,1,0:T(8,128)} %copy.700) | data formatting | bytes 16777216 | tf_op jit(solution)/shard_map/reshape | solution.py:49
  974.8 160.9 %reduce_sum.108 = f32[64,64,64]{2,1,0:T(8,128)} reduce(f32[64,2,64,2,64,2]{5,4,3,2,1,0:T(8,128)} %reshape.154, f32[]{:T(128)} %constant.46.clone.1), dimensions={1,3,5}, to_apply=%region_0.1 | reduce | flops 1835008 | bytes 9437188 | tf_op jit(solution)/shard_map/reduce_sum | solution.py:49
  1170.4 8.9 fusion.180
  1213.3 71.6 %reshape.155 = f32[32,2,32,2,32,2]{5,4,3,2,1,0:T(8,128)} reshape(f32[64,64,64]{2,1,0:T(8,128)} %fusion.172) | data formatting | bytes 2097152 | tf_op jit(solution)/shard_map/reshape | solution.py:49
  1284.9 20.8 reduce_sum.109
  1912.6 9.2 copy.767
  1921.9 9.3 copy.768
  1931.2 11.9 add.1655
  1943.1 13.2 fusion.670
  1987.1 16.0 negate_select_fusion.13
  2005.4 32.4 fusion.51
  2082.8 16.0 negate_select_fusion.11
  2101.0 32.4 fusion.43
  2133.5 8.1 fusion.664
  2178.1 16.0 negate_select_fusion.9
  2196.4 32.4 fusion.35
  2228.8 8.1 fusion.661
  2273.7 16.0 negate_select_fusion.7
  2292.0 32.4 fusion.27
  2324.4 8.1 fusion.658
  2369.1 16.0 negate_select_fusion.5
  2387.4 32.4 fusion.19
  2419.8 9.3 copy.790
  2429.1 538.7 %reshape.179 = f32[64,2,64,2,64,2]{5,4,3,2,1,0:T(8,128)} reshape(f32[128,128,128]{2,1,0:T(8,128)} %copy.790) | data formatting | bytes 16777216 | tf_op jit(solution)/shard_map/reshape | solution.py:49
  2967.8 160.9 %reduce_sum.114 = f32[64,64,64]{2,1,0:T(8,128)} reduce(f32[64,2,64,2,64,2]{5,4,3,2,1,0:T(8,128)} %reshape.179, f32[]{:T(128)} %constant.46.clone.1), dimensions={1,3,5}, to_apply=%region_6.7 | reduce | flops 1835008 | bytes 9437188 | tf_op jit(solution)/shard_map/reduce_sum | solution.py:49
  3161.8 8.9 fusion.142
  3204.3 71.6 %reshape.180 = f32[32,2,32,2,32,2]{5,4,3,2,1,0:T(8,128)} reshape(f32[64,64,64]{2,1,0:T(8,128)} %fusion.134) | data formatting | bytes 2097152 | tf_op jit(solution)/shard_map/reshape | solution.py:49
  3275.9 20.8 reduce_sum.115
  3897.2 9.2 copy.866
  3906.4 9.3 copy.867
  3915.7 11.9 add.1865
  3927.6 13.2 fusion.655
  3971.7 16.0 negate_select_fusion.3
  3990.0 32.4 fusion.11
  4067.4 16.0 negate_select_fusion.1
  4085.7 35.2 fusion.3
  4120.9 9.2 copy.876
  (1657 shorter events, 1854.5 us)
Async XLA Ops:
  0.0 153.0 %collective-permute-start.23 = (f32[64,64,1]{1,0,2:T(8,128)S(1)}, f32[64,64,1]{1,0,2:T(8,128)S(1)}, u32[]{:S(2)}, u32[]{:S(2)}) collective-permute-start(f32[64,64,1]{1,0,2:T(8,128)S(1)} %broadcast.403), channel_id=1, source_target_pairs={{1,0},{3,2},{5,4},{7,6}} | collective-permute-start | bytes 49160 | tf_op jit(solution)/shard_map/ppermute | solution.py:27
  1.4 158.3 %collective-permute-start.22 = (f32[64,64,1]{1,0,2:T(8,128)S(1)}, f32[64,64,1]{1,0,2:T(8,128)S(1)}, u32[]{:S(2)}, u32[]{:S(2)}) collective-permute-start(f32[64,64,1]{1,0,2:T(8,128)S(1)} %broadcast.403), channel_id=1, source_target_pairs={{0,1},{2,3},{4,5},{6,7}} | collective-permute-start | bytes 49160 | tf_op jit(solution)/shard_map/ppermute | solution.py:26
  4.5 158.7 %collective-permute-start.21 = (f32[64,1,64]{2,1,0:T(1,128)S(1)}, f32[64,1,64]{2,1,0:T(1,128)S(1)}, u32[]{:S(2)}, u32[]{:S(2)}) collective-permute-start(f32[64,1,64]{2,1,0:T(1,128)S(1)} %broadcast.401), channel_id=1, source_target_pairs={{2,0},{3,1},{6,4},{7,5}} | collective-permute-start | bytes 49160 | tf_op jit(solution)/shard_map/ppermute | solution.py:27
  5.8 159.3 %collective-permute-start.20 = (f32[64,1,64]{2,1,0:T(1,128)S(1)}, f32[64,1,64]{2,1,0:T(1,128)S(1)}, u32[]{:S(2)}, u32[]{:S(2)}) collective-permute-start(f32[64,1,64]{2,1,0:T(1,128)S(1)} %broadcast.401), channel_id=1, source_target_pairs={{0,2},{1,3},{4,6},{5,7}} | collective-permute-start | bytes 49160 | tf_op jit(solution)/shard_map/ppermute | solution.py:26
  10.9 45.9 %collective-permute-start.95 = (f32[4,4,1]{2,1,0:T(4,128)S(1)}, f32[4,4,1]{2,1,0:T(4,128)S(1)}, u32[]{:S(2)}, u32[]{:S(2)}) collective-permute-start(f32[4,4,1]{2,1,0:T(4,128)S(1)} %broadcast.443), channel_id=1, source_target_pairs={{1,0},{3,2},{5,4},{7,6}} | collective-permute-start | bytes 200 | tf_op jit(solution)/shard_map/ppermute | solution.py:27
  165.1 35.5 collective-permute-start.2
  170.0 30.6 collective-permute-start.3
  171.9 29.6 collective-permute-start.4
  173.8 27.7 collective-permute-start.5
  249.0 20.6 collective-permute-start.6
  261.3 35.2 collective-permute-start.8
  265.8 30.7 collective-permute-start.9
  267.1 30.3 collective-permute-start.10
  269.6 27.8 collective-permute-start.11
  356.9 35.2 collective-permute-start.14
  361.2 30.9 collective-permute-start.15
  362.5 30.5 collective-permute-start.16
  364.9 28.1 collective-permute-start.17
  1971.8 31.2 collective-permute-start.206
  1973.4 29.6 collective-permute-start.207
  1974.7 29.2 collective-permute-start.208
  1976.2 27.7 collective-permute-start.209
  2051.5 20.4 collective-permute-start.210
  2063.5 35.2 collective-permute-start.212
  2068.1 30.7 collective-permute-start.213
  2069.4 30.3 collective-permute-start.214
  2071.9 27.8 collective-permute-start.215
  2159.2 35.0 collective-permute-start.218
  2163.4 30.7 collective-permute-start.219
  2164.7 30.3 collective-permute-start.220
  2167.2 27.8 collective-permute-start.221
  2254.5 35.2 collective-permute-start.224
  2258.8 30.9 collective-permute-start.225
  2260.1 30.5 collective-permute-start.226
  2262.6 28.0 collective-permute-start.227
  2350.1 35.0 collective-permute-start.230
  2354.4 30.7 collective-permute-start.231
  2355.7 30.3 collective-permute-start.232
  2358.2 27.8 collective-permute-start.233
  3956.4 31.3 collective-permute-start.392
  3958.0 29.7 collective-permute-start.393
  3959.3 29.3 collective-permute-start.394
  3960.8 27.8 collective-permute-start.395
  4036.1 20.4 collective-permute-start.396
  4048.1 35.2 collective-permute-start.398
  4052.7 30.7 collective-permute-start.399
  4054.0 30.3 collective-permute-start.400
  4056.5 27.8 collective-permute-start.401
  (410 other events, 5803.4 us)
where the time goes:
time: 4150 us; the launch traced here: 4130 us
  local copies, waits for them, and re-layouts  1850 us (45%)
  other arithmetic  1120 us (27%)
  starting transfers between devices  906 us (22%)
  waiting for transfers between devices  215 us (5%)
    reshape x12, local copies, waits for them, and re-layouts, restrict(): fine_grid.reshape(dim_z // 2, 2, dim_y // 2, 2, dim_x // 2, 2)  1240 us
    ppermute x201, starting transfers between devices, with_ghosts(): lax.ppermute(last_face, axis_name, [(src_id, src_id + 1) for src_id in ra...  640 us
    reduce_sum x12, other arithmetic, restrict(): fine_grid.reshape(dim_z // 2, 2, dim_y // 2, 2, dim_x // 2, 2)  377 us
    add x38, other arithmetic, jacobi(): (1.0 - OMEGA) * iterate  301 us
    ppermute x201, starting transfers between devices, with_ghosts(): lax.ppermute(first_face, axis_name, [(src_id + 1, src_id) for src_id in r...  265 us
    select_n x201, other arithmetic, with_ghosts(): low_ghost = jnp.where(position == 0, -first_face, from_below)  238 us
    slice x206, local copies, waits for them, and re-layouts, with_ghosts(): last_face = lax.slice_in_dim(iterate, extent - 1, extent, axis=axis_id)  211 us
    ppermute x201, waiting for transfers between devices, with_ghosts(): lax.ppermute(first_face, axis_name, [(src_id + 1, src_id) for src_id in r...  203 us
  transfers between devices with their start and end apart: 402, of which 127 were waited for; matrix products, arithmetic and copies ran while one was open for 12% of the time, Pallas kernels for 0%

commit v1 on v0

v1 whole, which is shorter than its diff:
```python
import functools

import jax
import jax.numpy as jnp
from jax import lax
from jax.experimental import pallas as pl
from jax.experimental.pallas import tpu as pltpu
from jax.sharding import PartitionSpec as P

MESH = pl.DeviceIdType.MESH
F32 = jnp.float32
NINTH = 1.0 / 9.0
H = 6
G3 = 4
CYCLES = 2
DU, DF, DV = 3, 4, 5
SUB, LANES = 8, 128
NEAR, FAR = 0.75, 0.25
COARSE = 4
VREGS = 72
BLOCK0 = 136
BLOCK1 = 136
BLOCKP = 64


def _loop(lo, count, step, body):
    assert count % step == 0

    def run(i, carry):
        body(lo + i * step)
        return carry

    if count == step:
        body(lo)
    else:
        lax.fori_loop(0, count // step, run, 0)


def _iota(shape, axis):
    return lax.broadcasted_iota(jnp.int32, shape, len(shape) + axis)


def _ysum(load, lo, n, total, v, last_row=7):
    sub = _iota((v.shape[0], SUB, LANES), -2)
    if lo == 0:
        ym = jnp.where(sub == 0, -v[:, :SUB], pltpu.roll(v[:, :SUB], 1, 1))
        if n > SUB:
            ym = jnp.concatenate([ym, load(7, n - SUB)], axis=1)
    else:
        ym = load(lo - 1, n)
    if lo + n == total:
        yp = jnp.where(sub == last_row, -v[:, n - SUB :], pltpu.roll(v[:, n - SUB :], 7, 1))
        if n > SUB:
            yp = jnp.concatenate([load(lo + 1, n - SUB), yp], axis=1)
    else:
        yp = load(lo + 1, n)
    return ym + yp


def _blocks(total, size):
    return [(lo, min(size, total - lo)) for lo in range(0, total, size)]


def _planes0(src, f, z, u, emit, resid):
    total = src.shape[2]
    at, down, up = pl.ds(z, u), pl.ds(z - 1, u), pl.ds(z + 1, u)
    for lo, n in _blocks(total, BLOCK0):
        lane = _iota((u, n, LANES), -1)
        ends = (lane == 0, lane == 127)
        if resid:
            coef = tuple(jnp.where(e, 7.0, 6.0) for e in ends)
        else:
            coef = tuple(jnp.where(e, 2.0 * NINTH, 3.0 * NINTH) for e in ends)
        rows = pl.ds(lo, n)
        v = (src[0, at, rows, :], src[1, at, rows, :])
        x = (
            v[1] + jnp.where(ends[0], 0.0, pltpu.roll(v[1], 1, 2)),
            v[0] + jnp.where(ends[1], 0.0, pltpu.roll(v[0], 127, 2)),
        )
        for p in range(2):
            ys = _ysum(lambda r, m: src[p, at, pl.ds(r, m), :], lo, n, total, v[p])
            zs = src[p, down, rows, :] + src[p, up, rows, :]
            s = (x[p] + ys) + zs
            d = NINTH * (s - coef[p] * v[p]) if resid else coef[p] * v[p] + NINTH * s
            emit(p, lo, n, d + f[p, at, rows, :])


def _sweep0(src, dst, f, depth, n):
    lo, count = H - depth, n + 2 * depth
    step = min((SUB, 7, 6), key=lambda u: -(-count // u) * u)
    whole = -(-count // step) * step
    lo -= (whole - count) // 2

    def body(z):
        def emit(p, row, m, value):
            dst[p, pl.ds(z, step), pl.ds(row, m), :] = value

        _planes0(src, f, z, step, emit, False)

    _loop(lo, whole, step, body)


def _pairs(value):
    value = value.reshape(value.shape[0] // 2, 2, *value.shape[1:])
    return value[:, 0] + value[:, 1]


def _restrict0(src, f, coarse, tmp, yh, n):
    half = (src.shape[2] - SUB) // 2
    step = 4

    def body(zc):
        acc = {}

        def emit(p, lo, m, value):
            acc[lo] = (acc[lo][0] + value, m) if lo in acc else (value, m)

        _planes0(src, f, H + 2 * zc, 2 * step, emit, True)
        for lo, (value, m) in acc.items():
            tmp[pl.ds(0, step), pl.ds(lo, m), :] = _pairs(value)
        even = tmp[pl.ds(0, step), pl.ds(SUB * yh, half, stride=2), :]
        odd = tmp[pl.ds(0, step), pl.ds(SUB * yh + 1, half, stride=2), :]
        coarse[pl.ds(H + zc, step), pl.ds(pl.multiple_of(SUB * yh, SUB), half), :] = 0.5 * (even + odd)

    _loop(0, n // 2, step, body)


def _prolong_zy(coarse, zc, u, start, n, at_top, at_end, last_row=7):
    sub = _iota((2 * u, SUB, LANES), -2)

    def load(r, m):
        rows = pl.ds(r, m)
        c = NEAR * coarse[pl.ds(zc, u), rows, :]
        low = c + FAR * coarse[pl.ds(zc - 1, u), rows, :]
        high = c + FAR * coarse[pl.ds(zc + 1, u), rows, :]
        return jnp.stack([low, high], axis=1).reshape(2 * u, m, LANES)

    c = load(start, n)
    if at_top:
        cm = jnp.where(sub == 0, -c[:, :SUB], pltpu.roll(c[:, :SUB], 1, 1))
        if n > SUB:
            cm = jnp.concatenate([cm, load(start + 7, n - SUB)], axis=1)
    else:
        cm = load(start - 1, n)
    if at_end:
        cp = jnp.where(sub == last_row, -c[:, n - SUB :], pltpu.roll(c[:, n - SUB :], 7, 1))
        if n > SUB:
            cp = jnp.concatenate([load(start + 1, n - SUB), cp], axis=1)
    else:
        cp = load(start + 1, n)
    return NEAR * c + FAR * cm, NEAR * c + FAR * cp


def _y_parts(rows, offset, block):
    parts = []
    whole = rows // 16 * SUB
    for lo, n in _blocks(whole, block):
        end = lo + n == whole and rows % 16 == 0
        parts.append((offset + lo, n, 2 * lo, 2 * n, lo == 0, end, 0))
    if rows % 16:
        if rows == SUB:
            parts.append((offset, SUB, 0, SUB, True, True, 0))
        else:
            parts.append((offset + whole - 4, SUB, rows - SUB, SUB, False, True, SUB))
    return parts


def _prolong0(coarse, u, tmp, yh, depth, n):
    parts = _y_parts(u.shape[2], 4 * yh, BLOCKP)
    step = 2
    around = (depth + 1) // 2

    def body(zc):
        fine_at = pl.ds(H + 2 * (zc - H), 2 * step)
        for start, m, fine, count, top, end, skip in parts:
            pair = _prolong_zy(coarse, zc, step, start, m, top, end)
            lane = _iota((2 * step, m, LANES), -1)
            for parity in range(2):
                edge = lane == (0 if parity == 0 else 127)
                slots = pl.ds(2 * step * parity, 2 * step)
                for yc, c in enumerate(pair):
                    side = jnp.where(edge, -c, pltpu.roll(c, 1 if parity == 0 else 127, 2))
                    tmp[slots, pl.ds(fine - skip + yc, m, stride=2), :] = NEAR * c + FAR * side
                u[parity, fine_at, pl.ds(fine, count), :] += tmp[slots, pl.ds(fine, count), :]

    _loop(H - around, n // 2 + 2 * around, step, body)


def _planes(src, b, z, u, stride, emit, resid):
    total = src.shape[1]
    at = pl.ds(z, u)
    for lo, n in _blocks(total, BLOCK1):
        lane = _iota((u, n, LANES), -1)
        first, last = lane < stride, lane >= LANES - stride
        edge = jnp.where(first, 1.0, 0.0) + jnp.where(last, 1.0, 0.0)
        coef = 6.0 + edge if resid else (3.0 - edge) * NINTH
        rows = pl.ds(lo, n)
        v = src[at, rows, :]
        x = jnp.where(first, 0.0, pltpu.roll(v, stride, 2)) + jnp.where(last, 0.0, pltpu.roll(v, LANES - stride, 2))
        ys = _ysum(lambda r, m: src[at, pl.ds(r, m), :], lo, n, total, v)
        s = (x + ys) + (src[pl.ds(z - 1, u), rows, :] + src[pl.ds(z + 1, u), rows, :])
        d = NINTH * (s - coef * v) if resid else coef * v + NINTH * s
        emit(lo, n, d + b[at, rows, :])


def _sweep(src, dst, b, stride, lo, count):
    tiles = src.shape[1] // SUB
    step = max(u for u in range(1, count + 1) if count % u == 0 and u * tiles <= VREGS)

    def body(z):
        def emit(row, m, value):
            dst[pl.ds(z, step), pl.ds(row, m), :] = value

        _planes(src, b, z, step, stride, emit, False)

    _loop(lo, count, step, body)


def _restrict(src, b, stride, tmp, fine_lo, coarse, coarse_lo, count, fine_row, coarse_row, rows, step):
    def body(i):
        acc = {}

        def emit(lo, m, value):
            acc[lo] = (value, m)

        _planes(src, b, fine_lo + 2 * i, 2 * step, stride, emit, True)
        slots = pl.ds(0, step)
        for lo, (value, m) in acc.items():
            tmp[slots, pl.ds(lo, m), :] = _pairs(value)
        s = tmp[slots, pl.ds(fine_row, rows, stride=2), :] + tmp[slots, pl.ds(fine_row + 1, rows, stride=2), :]
        s = 0.5 * (s + pltpu.roll(s, LANES - stride, 2))
        row = coarse_row if isinstance(coarse_row, int) else pl.multiple_of(coarse_row, SUB)
        coarse[pl.ds(coarse_lo + i, step), pl.ds(row, rows), :] = s

    _loop(0, count, step, body)


def _prolong(coarse, v, stride, tmp, fine_lo, coarse_lo, count, offset, step, last_row=7):
    parts = _y_parts(v.shape[1], offset, BLOCKP)

    def body(i):
        fine_at = pl.ds(fine_lo + 2 * i, 2 * step)
        slots = pl.ds(0, 2 * step)
        for start, m, fine, n, top, end, skip in parts:
            lane = _iota((2 * step, m, LANES), -1)
            is_high = jnp.bitwise_and(lane, stride) != 0
            edge = (is_high & (lane >= LANES - 2 * stride)) | (jnp.logical_not(is_high) & (lane < 2 * stride))
            for yc, c in enumerate(_prolong_zy(coarse, coarse_lo + i, step, start, m, top, end, last_row)):
                own = jnp.where(is_high, pltpu.roll(c, stride, 2), c)
                side = jnp.where(is_high, pltpu.roll(c, LANES - stride, 2), pltpu.roll(c, 2 * stride, 2))
                side = jnp.where(edge, -own, side)
                tmp[slots, pl.ds(fine - skip + yc, m, stride=2), :] = NEAR * own + FAR * side
            v[fine_at, pl.ds(fine, n), :] += tmp[slots, pl.ds(fine, n), :]

    _loop(0, count, step, body)


def _mirror(ref, planes, ghost):
    def fill(k, carry=0):
        ref[ghost - 1 - k] = -ref[ghost + k]
        ref[ghost + planes + k] = -ref[ghost + planes - 1 - k]
        return carry

    if ghost == 1:
        fill(0)
    else:
        lax.fori_loop(0, ghost, fill, 0)


def _split_dot(x, m, left=False):
    hi = x.astype(jnp.bfloat16).astype(F32)
    rest = x - hi
    mid = rest.astype(jnp.bfloat16).astype(F32)
    low = rest - mid
    dot = functools.partial(jnp.dot, preferred_element_type=F32)
    if left:
        return (dot(m, hi) + dot(m, mid)) + dot(m, low)
    return (dot(hi, m) + dot(mid, m)) + dot(low, m)


def _kernel(u_in, f_in, inv, out, u0, u1, f, b1, v1a, v1b, b2, v2a, v2b, b3, v3a, v3b, b4, v4a, v4b, b5, v5a, v5b,
            b6, v6, tmp, send, recv, local):
    gz, gy, gx = (lax.axis_index(name) for name in ("gz", "gy", "gx"))
    zq, yh = 2 * gz + gx, gy
    core0, rows0 = u0.shape[1] - 2 * H, u0.shape[2] - SUB
    n1, n2, n3 = core0 // 2, core0 // 4, core0 // SUB
    r1, r2, r3 = rows0 // 2, rows0 // 4, rows0 // SUB
    counter = [0]

    def to(z, y, x):
        return {"gz": z, "gy": y, "gx": x}

    def remote(src, dst, slot, device):
        return pltpu.make_async_remote_copy(src_ref=src, dst_ref=dst, send_sem=send.at[slot], recv_sem=recv.at[slot],
                                            device_id=device, device_id_type=MESH)

    def new_slot():
        counter[0] += 1
        return counter[0] - 1

    barrier = pltpu.get_barrier_semaphore()
    others = [(a, b, c) for a in range(2) for b in range(2) for c in range(2) if a + b + c]
    for a, b, c in others:
        pl.semaphore_signal(barrier, inc=1, device_id=to(lax.rem(gz + a, 2), lax.rem(gy + b, 2), lax.rem(gx + c, 2)),
                            device_id_type=MESH)
    pl.semaphore_wait(barrier, len(others))

    def scatter(brick, window, d, lsem):
        waits = []
        n = core0 + d

        def mine(t):
            return brick.at[pl.ds(t * (core0 - d), n)]

        def place(half, t, row, count):
            return window.at[half, pl.ds(H - t * d, n), pl.ds(row, count)]

        row_src = pl.multiple_of((1 - gy) * (rows0 - SUB), SUB)
        row_dst = pl.multiple_of(gy * rows0, SUB)
        row_in = pl.multiple_of((1 - gy) * rows0, SUB)
        core_row = pl.multiple_of(SUB * gy, SUB)
        own = pltpu.make_async_copy(mine(gx), place(gx, gx, core_row, rows0), local.at[lsem])
        own.start()
        waits.append(own.wait)
        t_far = 1 - gz
        z_src = (1 - gz) * (LANES - d)
        z_dst = jnp.where(gz == 0, H - d, H + core0)
        z_in = jnp.where(gz == 0, H + core0, H - d)
        inner = gx == 1 - gz
        slots = {(kind, s): new_slot() for kind in ("z", "d") for s in range(2)}
        for s in range(2):
            cz = remote(brick.at[pl.ds(z_src, d)], window.at[s, pl.ds(z_dst, d), pl.ds(core_row, rows0)],
                        slots["z", s], to(1 - gz, gy, 1 - t_far))
            cd = remote(brick.at[pl.ds(z_src, d), pl.ds(row_src, SUB)], window.at[s, pl.ds(z_dst, d), pl.ds(row_dst, SUB)],
                        slots["d", s], to(1 - gz, 1 - gy, 1 - t_far))
            rz = remote(brick.at[pl.ds(z_src, d)], window.at[s, pl.ds(z_in, d), pl.ds(core_row, rows0)],
                        slots["z", s], to(1 - gz, gy, 1 - t_far))
            rd = remote(brick.at[pl.ds(z_src, d), pl.ds(row_src, SUB)], window.at[s, pl.ds(z_in, d), pl.ds(row_in, SUB)],
                        slots["d", s], to(1 - gz, 1 - gy, 1 - t_far))

            @pl.when(gx == s)
            def _():
                cz.start()
                cd.start()

            def wait(cz=cz, cd=cd, rz=rz, rd=rd, s=s):
                @pl.when(gx == s)
                def _():
                    cz.wait_send()
                    cd.wait_send()

                @pl.when(inner)
                def _():
                    rz.wait_recv()
                    rd.wait_recv()

            waits.append(wait)
        slots = {(s, t): new_slot() for s in range(2) for t in range(2)}
        for s in range(2):
            for t in range(2):
                cy = remote(brick.at[pl.ds(t * (core0 - d), n), pl.ds(row_src, SUB)], place(s, t, row_dst, SUB),
                            slots[s, t], to(gz, 1 - gy, t))
                ry = remote(brick.at[pl.ds(t * (core0 - d), n), pl.ds(row_src, SUB)], place(s, t, row_in, SUB),
                            slots[s, t], to(gz, 1 - gy, t))

                @pl.when(gx == s)
                def _():
                    cy.start()

                def wait(cy=cy, ry=ry, s=s, t=t):
                    @pl.when(gx == s)
                    def _():
                        cy.wait_send()

                    @pl.when(gx == t)
                    def _():
                        ry.wait_recv()

                waits.append(wait)
        slot = new_slot()
        cp = remote(mine(1 - gx), place(gx, 1 - gx, core_row, rows0), slot, to(gz, gy, 1 - gx))
        rp = remote(mine(gx), place(1 - gx, gx, core_row, rows0), slot, to(gz, gy, 1 - gx))
        cp.start()

        def wait():
            cp.wait_send()
            rp.wait_recv()

        waits.append(wait)
        return waits

    def reflect(ref, n, d, lead):
        def fill(dst, src):
            def step(k, carry):
                for p in range(lead):
                    r = ref.at[p] if lead > 1 else ref
                    r[dst(k)] = -r[src(k)]
                return carry

            lax.fori_loop(0, d, step, 0)

        @pl.when(zq == 0)
        def _():
            fill(lambda k: H - 1 - k, lambda k: H + k)

        @pl.when(zq == 3)
        def _():
            fill(lambda k: H + n + k, lambda k: H + n - 1 - k)

    def exchange(ref, n, m, d, lead):
        pre = (slice(None),) if lead > 1 else ()

        def at(z, dz, row, dr):
            return ref.at[pre + (pl.ds(z, dz), pl.ds(pl.multiple_of(row, SUB), dr))]

        core_row = SUB * yh
        row_src = (1 - yh) * (m - SUB) + yh * SUB
        row_dst = yh * m
        row_in = (1 - yh) * m
        waits = []
        slot = new_slot()
        across = remote(at(H, n, row_src, SUB), at(H, n, row_dst, SUB), slot, to(gz, 1 - gy, gx))
        arrive = remote(at(H, n, row_src, SUB), at(H, n, row_in, SUB), slot, to(gz, 1 - gy, gx))
        jobs = []
        for up in (False, True):
            qz = jnp.minimum(gz + gx, 1) if up else jnp.maximum(gz + gx - 1, 0)
            qx = 1 - gx
            z_src = H + n - d if up else H
            z_dst = H - d if up else H + n
            z_in = H - d if up else H + n
            sends = zq < 3 if up else zq > 0
            takes = zq > 0 if up else zq < 3
            sz, sd = new_slot(), new_slot()
            cz = remote(at(z_src, d, core_row, m), at(z_dst, d, core_row, m), sz, to(qz, gy, qx))
            cd = remote(at(z_src, d, row_src, SUB), at(z_dst, d, row_dst, SUB), sd, to(qz, 1 - gy, qx))
            rz = remote(at(z_src, d, core_row, m), at(z_in, d, core_row, m), sz, to(qz, gy, qx))
            rd = remote(at(z_src, d, row_src, SUB), at(z_in, d, row_in, SUB), sd, to(qz, 1 - gy, qx))
            jobs.append((sends, takes, cz, cd, rz, rd))
        for sends, _, cz, cd, _, _ in jobs:

            @pl.when(sends)
            def _():
                cd.start()
                cz.start()

        across.start()

        def wait():
            across.wait_send()
            arrive.wait_recv()
            for sends, takes, cz, cd, rz, rd in jobs:

                @pl.when(sends)
                def _():
                    cz.wait_send()
                    cd.wait_send()

                @pl.when(takes)
                def _():
                    rz.wait_recv()
                    rd.wait_recv()

        waits.append(wait)
        return wait

    waits_u = scatter(u_in, u0, DU, 0)
    waits_f = scatter(f_in, f, DF, 1)

    col = lax.broadcasted_iota(jnp.int32, (256, 256), 1)
    row = lax.broadcasted_iota(jnp.int32, (256, 256), 0)
    split = (row == 2 * jnp.bitwise_and(col, 127) + lax.shift_right_logical(col, 7)).astype(F32)
    merge = (col == 2 * jnp.bitwise_and(row, 127) + lax.shift_right_logical(row, 7)).astype(F32)
    def lanes(shape, axis, sign):
        cell = lax.broadcasted_iota(jnp.int32, shape, 1 - axis)
        spot = lax.broadcasted_iota(jnp.int32, shape, axis)
        z = lax.shift_right_logical(cell, 4)
        y = jnp.bitwise_and(lax.shift_right_logical(cell, 2), 3)
        x = jnp.bitwise_and(cell, 3)
        return (spot == jnp.bitwise_and(32 * x + sign * (4 * z + y), 127)).astype(F32)

    table = _split_dot(_split_dot(inv[...], lanes((64, LANES), 1, -1)), lanes((LANES, 64), 0, 1), left=True) * (9.0 * 16.0)

    for wait in waits_u:
        wait()

    def permute(ref, m, scale, lo, count, dst):
        def body(z):
            for k in range(2):
                x = jnp.concatenate([ref[0, z + k], ref[1, z + k]], axis=1)
                y = _split_dot(x, m)
                if scale is not None:
                    y = y * scale
                dst[0, z + k] = y[:, :LANES]
                dst[1, z + k] = y[:, LANES:]

        _loop(lo, count, 2, body)

    reflect(u0, core0, DU, 2)
    permute(u0, split, None, H - DU, core0 + 2 * DU, u0)
    for wait in waits_f:
        wait()
    reflect(f, core0, DF, 2)
    permute(f, split, NINTH / 65536.0, H - DF, core0 + 2 * DF, f)

    def bottom():
        lane, sub = _iota(v6.shape[1:], -1), _iota(v6.shape[1:], -2)
        valid = jnp.bitwise_and(lane, 31) == 0
        total = jnp.zeros(v6.shape[1:], F32)
        for i in range(COARSE * COARSE):
            z, y = divmod(i, COARSE)
            total = total + pltpu.roll(jnp.where(valid & (sub == y), b6[z], 0.0), i, 1)
        for shift in (4, 2, 1):
            total = total + pltpu.roll(total, shift, 0)
        e6 = jnp.dot(total, table, precision=lax.Precision.HIGHEST, preferred_element_type=F32)
        for z in range(COARSE):
            plane = e6
            for y in range(COARSE):
                plane = jnp.where(sub == y, pltpu.roll(e6, COARSE * z + y, 1), plane)
            v6[1 + z] = plane
        _mirror(v6, COARSE, 1)

    for cycle in range(CYCLES):
        c1, c2, c3 = b1.at[cycle], b2.at[cycle], b3.at[cycle]
        more = cycle + 1 < CYCLES
        if cycle == 0:
            _sweep0(u0, u1, f, 2, core0)
            _sweep0(u1, u0, f, 1, core0)
        _restrict0(u0, f, c1, tmp, yh, core0)
        wait_b1 = exchange(c1, n1, r1, H, 1)
        wait_b1()
        reflect(c1, n1, H, 1)
        _sweep(c1, v1a, c1, 1, 1, c1.shape[0] - 2)
        _restrict(v1a, c1, 1, tmp, H, c2, H, n2, SUB * yh, SUB * yh, r2, 4)
        wait_b2 = exchange(c2, n2, r2, H, 1)
        wait_b2()
        reflect(c2, n2, H, 1)
        _sweep(c2, v2a, c2, 2, 1, c2.shape[0] - 2)
        _restrict(v2a, c2, 2, tmp, H, c3, G3 + n3 * zq, n3, SUB * yh, r3 * yh, r3, 4)
        waits3 = []

        def block(z, y, x):
            return c3.at[pl.ds(G3 + n3 * (2 * z + x), n3), pl.ds(pl.multiple_of(r3 * y, SUB), r3)]

        for a, b, c in others:
            z, y, x = lax.rem(gz + a, 2), lax.rem(gy + b, 2), lax.rem(gx + c, 2)
            slot = new_slot()
            src = block(gz, gy, gx)
            give = remote(src, src, slot, to(z, y, x))
            take = remote(src, block(z, y, x), slot, to(z, y, x))
            give.start()
            waits3.append((give, take))
        for give, take in waits3:
            give.wait_send()
            take.wait_recv()
        depth = DV if more else 2
        wait_v = exchange(u0, core0, rows0, depth, 2)
        small = ((4, G3, c3, v3a, v3b), (SUB, 1, b4, v4a, v4b), (16, 1, b5, v5a, v5b))
        after = ((b4, 1), (b5, 1), (b6, 0))
        for (stride, g, b, va, vb), (coarse, ghost) in zip(small, after):
            n = b.shape[0] - 2 * g
            _mirror(b, n, g)
            _sweep(b, va, b, stride, g, n)
            _mirror(va, n, g)
            _restrict(va, b, stride, tmp, g, coarse, ghost, n // 2, 0, 0, coarse.shape[1], 4)
        bottom()
        coarse, last_row = v6, COARSE - 1
        for stride, g, b, va, vb in reversed(small):
            n = b.shape[0] - 2 * g
            _prolong(coarse, va, stride, tmp, g, 1, n // 2, 0, 4, last_row)
            _mirror(va, n, g)
            _sweep(va, vb, b, stride, g, n)
            _mirror(vb, n, g)
            _sweep(vb, va, b, stride, g, n)
            _mirror(va, n, g)
            coarse, last_row = va, SUB - 1
        half = H // 2
        _prolong(v3a, v2a, 2, tmp, 0, G3 + n3 * zq - half, n3 + H, (r3 - 4) * yh, 2)
        _sweep(v2a, v2b, c2, 2, 2, c2.shape[0] - 4)
        _sweep(v2b, v2a, c2, 2, 2, c2.shape[0] - 4)
        _prolong(v2a, v1a, 1, tmp, 0, half, n2 + H, 4 * yh, 2)
        _sweep(v1a, v1b, c1, 1, 2, c1.shape[0] - 4)
        _sweep(v1b, v1a, c1, 1, 2, c1.shape[0] - 4)
        wait_v()
        reflect(u0, core0, depth, 2)
        _prolong0(v1a, u0, tmp, yh, depth, core0)
        for left in reversed(range(0, depth - 1 if more else depth, 2)):
            _sweep0(u0, u1, f, left + 1 + more, core0)
            _sweep0(u1, u0, f, left + more, core0)

    permute(u0, merge, None, H, core0, u1)
    core_row = pl.multiple_of(SUB * yh, SUB)

    def part(half):
        return u1.at[half, pl.ds(H, core0), pl.ds(core_row, rows0)]

    slot = new_slot()
    keep = pltpu.make_async_copy(part(gx), out.at[pl.ds(core0 * gx, core0)], local.at[2])
    give = remote(part(1 - gx), out.at[pl.ds(core0 * gx, core0)], slot, to(gz, gy, 1 - gx))
    take = remote(part(1 - gx), out.at[pl.ds(core0 * (1 - gx), core0)], slot, to(gz, gy, 1 - gx))
    give.start()
    keep.start()
    keep.wait()
    give.wait_send()
    take.wait_recv()


SLOTS = 80


def solution(mesh):
    spec = P(("batch", "gz"), "gy", "gx")

    def local(rhs, init, inv):
        def vm(*shape):
            return pltpu.VMEM(shape, F32)

        def level(planes, rows, *lead):
            return [vm(*lead, planes, rows, LANES), vm(planes, rows, LANES), vm(planes, rows, LANES)]

        nz, ny = init.shape[0] // 2, init.shape[1]
        scratch = [vm(2, nz + 2 * H, ny + SUB, LANES)] * 3
        for l in (1, 2):
            scratch += level((nz >> l) + 2 * H, (ny >> l) + SUB, CYCLES)
        scratch += level(nz // 2 + 2 * G3, nz // 2, CYCLES)
        scratch += level(nz // 4 + 2, nz // 4) + level(nz // SUB + 2, SUB)
        scratch += [vm(COARSE, SUB, LANES), vm(COARSE + 2, SUB, LANES), vm(16, ny + 3 * SUB, LANES)]
        sems = pltpu.SemaphoreType.DMA((SLOTS,))
        call = pl.pallas_call(
            _kernel,
            out_shape=jax.ShapeDtypeStruct(init.shape, F32),
            in_specs=[pl.BlockSpec(memory_space=pl.ANY)] * 2 + [pl.BlockSpec(memory_space=pltpu.VMEM)],
            out_specs=pl.BlockSpec(memory_space=pl.ANY),
            scratch_shapes=scratch + [sems] * 3,
            compiler_params=pltpu.CompilerParams(
                collective_id=0, has_side_effects=True, vmem_limit_bytes=62 * 2**20
            ),
            name="vcycles",
        )
        return call(init, rhs, inv)

    return jax.shard_map(local, mesh=mesh, in_specs=(spec, spec, P()), out_specs=spec, check_vma=False)
```

time: 4150 us -> 194 us (0.05)
  local copies, waits for them, and re-layouts: 1850 us -> 7.89 us
  other arithmetic: 1120 us -> 0 us
  starting transfers between devices: 906 us -> 0 us
  waiting for transfers between devices: 215 us -> 0 us
  Pallas kernels: 0 us -> 186 us
    reshape x29 -> x0, local copies, waits for them, and re-layouts: 1280 us -> none  [the longest x12 1240 us: restrict(): fine_grid.reshape(dim_z // 2, 2, dim_y // 2, 2, dim_x // 2, 2)]
    ppermute x402 -> x0, starting transfers between devices: 906 us -> none  [the longest x201 640 us: with_ghosts(): lax.ppermute(last_face, axis_name, [(src_id, src_id + 1) for src_id in ra...]
    reduce_sum x12 -> x0, other arithmetic: 377 us -> none  [restrict(): fine_grid.reshape(dim_z // 2, 2, dim_y // 2, 2, dim_x // 2, 2)]
    add x54 -> x0, other arithmetic: 335 us -> none  [the longest x38 301 us: jacobi(): (1.0 - OMEGA) * iterate]
    slice x226 -> x0, local copies, waits for them, and re-layouts: 281 us -> none  [the longest x206 211 us: with_ghosts(): last_face = lax.slice_in_dim(iterate, extent - 1, extent, axis=axis_id)]
    select_n x226 -> x0, other arithmetic: 266 us -> none  [the longest x201 238 us: with_ghosts(): low_ghost = jnp.where(position == 0, -first_face, from_below)]
    ppermute x402 -> x0, waiting for transfers between devices: 215 us -> none  [the longest x201 203 us: with_ghosts(): lax.ppermute(first_face, axis_name, [(src_id + 1, src_id) for src_id in r...]
    pallas_call x0 -> x1, Pallas kernels: none -> 186 us  [local(): return call(init, rhs, inv)]
  transfers between devices with their start and end apart: 402 -> 0, of which waited for: 127 -> 0; matrix products, arithmetic and copies ran while one was open for 12% -> 0% of each run, Pallas kernels for 0% -> 0%
where the time goes in v1:
time: 194 us
  Pallas kernels  186 us (96%)
  local copies, waits for them, and re-layouts  7.89 us (4%)
    pallas_call x1, Pallas kernels, local(): return call(init, rhs, inv)  186 us
    unnamed x1, local copies, waits for them, and re-layouts  7.89 us

profile of v1, /device:TPU:0, one launch (start us, length us, event | category | flops | bytes accessed | tf_op | source)
XLA Modules:
  0.0 193.5 jit_solution(3937410284927748021)
XLA Ops:
  0.0 185.6 %vcycles.1 = f32[128,128,128]{2,1,0:T(8,128)} custom-call(f32[128,128,128]{2,1,0:T(8,128)} %u_in.1, f32[128,128,128]{2,1,0:T(8,128)} %f_in.1, f32[64,64]{1,0:T(8,128)} %inv.1), custom_call_target="tpu_custom_call" | custom-call | tf_op jit(solution)/shard_map/vcycles/pallas_call | solution.py:639
  185.6 7.9 %copy.5 = f32[128,128,128]{2,1,0:T(8,128)} copy(f32[128,128,128]{2,1,0:T(8,128)} %vcycles.1) | data formatting | bytes 16777216

commit v2 on v1

--- a/solution.py
+++ b/solution.py
@@ -18,6 +18,7 @@
 NEAR, FAR = 0.75, 0.25
 COARSE = 4
 VREGS = 72
+PERMUTE = 8
 BLOCK0 = 136
 BLOCK1 = 136
 BLOCKP = 64
@@ -305,6 +306,10 @@
                             device_id_type=MESH)
     pl.semaphore_wait(barrier, len(others))
 
+    def seam(m, d, start):
+        below = SUB - d
+        return (1 - yh) * (m - d) + yh * start, (1 - yh) * below + yh * m, yh * below + (1 - yh) * m
+
     def scatter(brick, window, d, lsem):
         waits = []
         n = core0 + d
@@ -315,9 +320,7 @@
         def place(half, t, row, count):
             return window.at[half, pl.ds(H - t * d, n), pl.ds(row, count)]
 
-        row_src = pl.multiple_of((1 - gy) * (rows0 - SUB), SUB)
-        row_dst = pl.multiple_of(gy * rows0, SUB)
-        row_in = pl.multiple_of((1 - gy) * rows0, SUB)
+        row_src, row_dst, row_in = seam(rows0, d, 0)
         core_row = pl.multiple_of(SUB * gy, SUB)
         own = pltpu.make_async_copy(mine(gx), place(gx, gx, core_row, rows0), local.at[lsem])
         own.start()
@@ -331,11 +334,11 @@
         for s in range(2):
             cz = remote(brick.at[pl.ds(z_src, d)], window.at[s, pl.ds(z_dst, d), pl.ds(core_row, rows0)],
                         slots["z", s], to(1 - gz, gy, 1 - t_far))
-            cd = remote(brick.at[pl.ds(z_src, d), pl.ds(row_src, SUB)], window.at[s, pl.ds(z_dst, d), pl.ds(row_dst, SUB)],
+            cd = remote(brick.at[pl.ds(z_src, d), pl.ds(row_src, d)], window.at[s, pl.ds(z_dst, d), pl.ds(row_dst, d)],
                         slots["d", s], to(1 - gz, 1 - gy, 1 - t_far))
             rz = remote(brick.at[pl.ds(z_src, d)], window.at[s, pl.ds(z_in, d), pl.ds(core_row, rows0)],
                         slots["z", s], to(1 - gz, gy, 1 - t_far))
-            rd = remote(brick.at[pl.ds(z_src, d), pl.ds(row_src, SUB)], window.at[s, pl.ds(z_in, d), pl.ds(row_in, SUB)],
+            rd = remote(brick.at[pl.ds(z_src, d), pl.ds(row_src, d)], window.at[s, pl.ds(z_in, d), pl.ds(row_in, d)],
                         slots["d", s], to(1 - gz, 1 - gy, 1 - t_far))
 
             @pl.when(gx == s)
@@ -358,9 +361,9 @@
         slots = {(s, t): new_slot() for s in range(2) for t in range(2)}
         for s in range(2):
             for t in range(2):
-                cy = remote(brick.at[pl.ds(t * (core0 - d), n), pl.ds(row_src, SUB)], place(s, t, row_dst, SUB),
+                cy = remote(brick.at[pl.ds(t * (core0 - d), n), pl.ds(row_src, d)], place(s, t, row_dst, d),
                             slots[s, t], to(gz, 1 - gy, t))
-                ry = remote(brick.at[pl.ds(t * (core0 - d), n), pl.ds(row_src, SUB)], place(s, t, row_in, SUB),
+                ry = remote(brick.at[pl.ds(t * (core0 - d), n), pl.ds(row_src, d)], place(s, t, row_in, d),
                             slots[s, t], to(gz, 1 - gy, t))
 
                 @pl.when(gx == s)
@@ -411,16 +414,14 @@
         pre = (slice(None),) if lead > 1 else ()
 
         def at(z, dz, row, dr):
-            return ref.at[pre + (pl.ds(z, dz), pl.ds(pl.multiple_of(row, SUB), dr))]
-
-        core_row = SUB * yh
-        row_src = (1 - yh) * (m - SUB) + yh * SUB
-        row_dst = yh * m
-        row_in = (1 - yh) * m
+            return ref.at[pre + (pl.ds(z, dz), pl.ds(row, dr))]
+
+        core_row = pl.multiple_of(SUB * yh, SUB)
+        row_src, row_dst, row_in = seam(m, d, SUB)
         waits = []
         slot = new_slot()
-        across = remote(at(H, n, row_src, SUB), at(H, n, row_dst, SUB), slot, to(gz, 1 - gy, gx))
-        arrive = remote(at(H, n, row_src, SUB), at(H, n, row_in, SUB), slot, to(gz, 1 - gy, gx))
+        across = remote(at(H, n, row_src, d), at(H, n, row_dst, d), slot, to(gz, 1 - gy, gx))
+        arrive = remote(at(H, n, row_src, d), at(H, n, row_in, d), slot, to(gz, 1 - gy, gx))
         jobs = []
         for up in (False, True):
             qz = jnp.minimum(gz + gx, 1) if up else jnp.maximum(gz + gx - 1, 0)
@@ -432,9 +433,9 @@
             takes = zq > 0 if up else zq < 3
             sz, sd = new_slot(), new_slot()
             cz = remote(at(z_src, d, core_row, m), at(z_dst, d, core_row, m), sz, to(qz, gy, qx))
-            cd = remote(at(z_src, d, row_src, SUB), at(z_dst, d, row_dst, SUB), sd, to(qz, 1 - gy, qx))
+            cd = remote(at(z_src, d, row_src, d), at(z_dst, d, row_dst, d), sd, to(qz, 1 - gy, qx))
             rz = remote(at(z_src, d, core_row, m), at(z_in, d, core_row, m), sz, to(qz, gy, qx))
-            rd = remote(at(z_src, d, row_src, SUB), at(z_in, d, row_in, SUB), sd, to(qz, 1 - gy, qx))
+            rd = remote(at(z_src, d, row_src, d), at(z_in, d, row_in, d), sd, to(qz, 1 - gy, qx))
             jobs.append((sends, takes, cz, cd, rz, rd))
         for sends, _, cz, cd, _, _ in jobs:
 
@@ -484,16 +485,18 @@
         wait()
 
     def permute(ref, m, scale, lo, count, dst):
+        step = max(u for u in range(1, PERMUTE + 1) if count % u == 0)
+
         def body(z):
-            for k in range(2):
-                x = jnp.concatenate([ref[0, z + k], ref[1, z + k]], axis=1)
-                y = _split_dot(x, m)
-                if scale is not None:
-                    y = y * scale
-                dst[0, z + k] = y[:, :LANES]
-                dst[1, z + k] = y[:, LANES:]
-
-        _loop(lo, count, 2, body)
+            at = pl.ds(z, step)
+            x = jnp.concatenate([ref[0, at], ref[1, at]], axis=-1)
+            y = _split_dot(x.reshape(-1, 2 * LANES), m).reshape(x.shape)
+            if scale is not None:
+                y = y * scale
+            dst[0, at] = y[..., :LANES]
+            dst[1, at] = y[..., LANES:]
+
+        _loop(lo, count, step, body)
 
     reflect(u0, core0, DU, 2)
     permute(u0, split, None, H - DU, core0 + 2 * DU, u0)
@@ -587,19 +590,22 @@
             _sweep0(u0, u1, f, left + 1 + more, core0)
             _sweep0(u1, u0, f, left + more, core0)
 
-    permute(u0, merge, None, H, core0, u1)
     core_row = pl.multiple_of(SUB * yh, SUB)
-
-    def part(half):
-        return u1.at[half, pl.ds(H, core0), pl.ds(core_row, rows0)]
-
     slot = new_slot()
-    keep = pltpu.make_async_copy(part(gx), out.at[pl.ds(core0 * gx, core0)], local.at[2])
-    give = remote(part(1 - gx), out.at[pl.ds(core0 * gx, core0)], slot, to(gz, gy, 1 - gx))
-    take = remote(part(1 - gx), out.at[pl.ds(core0 * (1 - gx), core0)], slot, to(gz, gy, 1 - gx))
+    here, there = pl.ds(core0 * gx, core0), pl.ds(core0 * (1 - gx), core0)
+    give = remote(u1.at[0, pl.ds(0, core0), pl.ds(0, rows0)], out.at[here], slot, to(gz, gy, 1 - gx))
+    take = remote(u1.at[0, pl.ds(0, core0), pl.ds(0, rows0)], out.at[there], slot, to(gz, gy, 1 - gx))
+
+    def unsplit(z):
+        at, rows = pl.ds(H + z, PERMUTE), pl.ds(core_row, rows0)
+        x = jnp.concatenate([u0[0, at, rows], u0[1, at, rows]], axis=-1)
+        y = _split_dot(x.reshape(-1, 2 * LANES), merge).reshape(x.shape)
+        low, high = y[..., :LANES], y[..., LANES:]
+        out[pl.ds(core0 * gx + z, PERMUTE)] = jnp.where(gx == 0, low, high)
+        u1[0, pl.ds(z, PERMUTE), pl.ds(0, rows0)] = jnp.where(gx == 0, high, low)
+
+    _loop(0, core0, PERMUTE, unsplit)
     give.start()
-    keep.start()
-    keep.wait()
     give.wait_send()
     take.wait_recv()
 
@@ -627,12 +633,12 @@
         sems = pltpu.SemaphoreType.DMA((SLOTS,))
         call = pl.pallas_call(
             _kernel,
-            out_shape=jax.ShapeDtypeStruct(init.shape, F32),
+            out_shape=pltpu.VMEM(init.shape, F32),
             in_specs=[pl.BlockSpec(memory_space=pl.ANY)] * 2 + [pl.BlockSpec(memory_space=pltpu.VMEM)],
-            out_specs=pl.BlockSpec(memory_space=pl.ANY),
+            out_specs=pl.BlockSpec(memory_space=pltpu.VMEM),
             scratch_shapes=scratch + [sems] * 3,
             compiler_params=pltpu.CompilerParams(
-                collective_id=0, has_side_effects=True, vmem_limit_bytes=62 * 2**20
+                collective_id=0, has_side_effects=True, vmem_limit_bytes=54 * 2**20
             ),
             name="vcycles",
         )

time: 194 us -> 164 us (0.85)
  Pallas kernels: 186 us -> 160 us
  local copies, waits for them, and re-layouts: 7.89 us -> 3.4 us
    pallas_call x1, Pallas kernels: 186 us -> 160 us  [local(): return call(init, rhs, inv)]
    unnamed x1, local copies, waits for them, and re-layouts: 7.89 us -> 3.4 us
where the time goes in v2:
time: 164 us
  Pallas kernels  160 us (98%)
  local copies, waits for them, and re-layouts  3.4 us (2%)
    pallas_call x1, Pallas kernels, local(): return call(init, rhs, inv)  160 us
    unnamed x1, local copies, waits for them, and re-layouts  3.4 us

profile of v2, /device:TPU:0, one launch (start us, length us, event | category | flops | bytes accessed | tf_op | source)
XLA Modules:
  0.0 163.6 jit_solution(7984747236847947300)
XLA Ops:
  0.0 160.2 %vcycles.1 = f32[128,128,128]{2,1,0:T(8,128)S(1)} custom-call(f32[128,128,128]{2,1,0:T(8,128)} %u_in.1, f32[128,128,128]{2,1,0:T(8,128)} %f_in.1, f32[64,64]{1,0:T(8,128)} %inv.1), custom_call_target="tpu_custom_call" | custom-call | tf_op jit(solution)/shard_map/vcycles/pallas_call | solution.py:645
  160.2 3.4 %copy.5 = f32[128,128,128]{2,1,0:T(8,128)} copy(f32[128,128,128]{2,1,0:T(8,128)S(1)} %vcycles.1) | data formatting | bytes 16777216
